TPU v7x, 32 devices: a whole 2x2x4 slice. The times are simulated.
32 devices in a mesh: rep: 8 (over z, core), tp: 4 (over y, x).
Axes of the slice: x: 2, y: 2, z: 4, core: 2. Of those that a mesh axis runs over, the one named last changes fastest.
Arguments:
- hidden_state: bfloat16 [32, 3584], P('rep'), may hold values from -6 to 6
- lengths: int32 [32], P('rep'), may hold values from 1 to 2048, as said below
- old_qkv: bfloat16 [3584, 4608], P(None, 'tp'), may hold values from -0.09375 to 0.09375
- old_out: bfloat16 [3584, 3584], P(None, 'tp'), may hold values from -0.09375 to 0.09375
- cache_keys: bfloat16 [32, 2048, 512], P('rep', 'tp'), may hold values from -64 to 64
- cache_values: bfloat16 [32, 2048, 512], P('rep', 'tp'), may hold values from -6 to 6
- new_qkv: bfloat16 [3584, 4608], P(('rep', 'tp')), may hold values from -0.09375 to 0.09375
- new_out: bfloat16 [3584, 3584], P(('rep', 'tp')), may hold values from -0.09375 to 0.09375
Outputs:
- decoded: bfloat16 [32, 3584], P('rep', 'tp')
- resharded_qkv: bfloat16 [3584, 4608], P(None, 'tp')
- resharded_out: bfloat16 [3584, 3584], P(None, 'tp')
Inputs may be any that keep to these rules, and one draw needn't show every extreme that they name: Every sequence has 1 to 2048 cached tokens, held in positions 0 to lengths - 1; in every draw some sequence fills its cache.
All inputs are finite; a program needn't handle non-finite values.
Results may differ from a plain program's by a relative error of at most 0.012.
Values may be sent and summed in bfloat16 or wider, within the bound.
A program may use at most 128 MiB of HBM per device.

v0:
```python
import jax
import jax.numpy as jnp
from jax import lax
from jax.sharding import PartitionSpec as P

HQ = 28
KVH = 4
HD = 128


ROPE_BASE = 1000000.0


def rotate(vectors, positions):
    half_dim = vectors.shape[-1] // 2
    frequency = ROPE_BASE ** (-2.0 * jnp.arange(half_dim, dtype=jnp.float32) / (2 * half_dim))
    angles = positions.astype(jnp.float32)[:, None, None] * frequency
    first_half = vectors[..., :half_dim]
    second_half = vectors[..., half_dim:]
    return jnp.concatenate(
        [
            first_half * jnp.cos(angles) - second_half * jnp.sin(angles),
            second_half * jnp.cos(angles) + first_half * jnp.sin(angles),
        ],
        axis=-1,
    )


def per_device(hidden_state, lengths, old_qkv, old_out, cache_keys, cache_values, new_qkv, new_out):
    pieces = (
        lax.all_to_all(new_qkv, "tp", split_axis=1, concat_axis=0, tiled=True),
        lax.all_to_all(new_out, "tp", split_axis=1, concat_axis=0, tiled=True),
    )
    qkv_tp, out_tp = (
        lax.all_gather(pieces[0], "rep", axis=0, tiled=True),
        lax.all_gather(pieces[1], "rep", axis=0, tiled=True),
    )
    seq_count = hidden_state.shape[0]
    local_joined = jnp.dot(hidden_state, old_qkv, preferred_element_type=jnp.float32).astype(
        jnp.bfloat16
    )
    joined_rows = lax.all_gather(local_joined, "tp", axis=1, tiled=True)
    q_width = HQ * HD
    k_width = KVH * HD
    group_size = HQ // KVH
    queries = rotate(
        joined_rows[:, :q_width].astype(jnp.float32).reshape(seq_count, HQ, HD), lengths
    ).astype(jnp.bfloat16)
    own_keys = rotate(
        joined_rows[:, q_width : q_width + k_width].astype(jnp.float32).reshape(seq_count, KVH, HD),
        lengths,
    ).astype(jnp.bfloat16)
    own_values = joined_rows[:, q_width + k_width :].reshape(seq_count, KVH, HD)
    inv_root = 1.0 / jnp.sqrt(jnp.float32(HD))
    cache_rows = cache_keys.shape[1]
    grouped = queries.reshape(seq_count, KVH, group_size, HD)
    key_blocks = cache_keys.reshape(seq_count, cache_rows, KVH, HD)
    value_blocks = cache_values.reshape(seq_count, cache_rows, KVH, HD)
    scores = (
        jnp.einsum("skgd,stkd->skgt", grouped, key_blocks, preferred_element_type=jnp.float32)
        * inv_root
    )
    positions = lax.axis_index("tp") * cache_rows + jnp.arange(cache_rows, dtype=jnp.int32)
    live_mask = (positions[None, :] < lengths[:, None])[:, None, None, :]
    scores = jnp.where(live_mask, scores, jnp.float32(-1e30))
    own_score = (
        jnp.sum(grouped.astype(jnp.float32) * own_keys.astype(jnp.float32)[:, :, None, :], axis=-1)
        * inv_root
    )
    local_top = jnp.maximum(jnp.max(scores, axis=-1), own_score)
    top_score = lax.pmax(local_top, "tp")
    weights = jnp.where(live_mask, jnp.exp(scores - top_score[..., None]), jnp.float32(0.0)).astype(
        jnp.bfloat16
    )
    numer_part = jnp.einsum(
        "skgt,stkd->skgd", weights, value_blocks, preferred_element_type=jnp.float32
    )
    denom_part = jnp.sum(weights.astype(jnp.float32), axis=-1)
    numerator, denominator = lax.psum((numer_part, denom_part), "tp")
    own_weight = lax.optimization_barrier(
        jnp.exp(own_score - top_score).astype(jnp.bfloat16)
    ).astype(jnp.float32)
    numerator = numerator + own_weight[..., None] * own_values.astype(jnp.float32)[:, :, None, :]
    denominator = denominator + own_weight
    attended = (numerator / denominator[..., None]).reshape(seq_count, q_width).astype(jnp.bfloat16)
    decoded = jnp.dot(attended, old_out, preferred_element_type=jnp.float32).astype(jnp.bfloat16)
    return (decoded, qkv_tp, out_tp)


def solution(mesh):
    in_specs = (
        P("rep", None),
        P("rep"),
        P(None, "tp"),
        P(None, "tp"),
        P("rep", "tp", None),
        P("rep", "tp", None),
        P(("rep", "tp"), None),
        P(("rep", "tp"), None),
    )
    out_specs = (P("rep", "tp"), P(None, "tp"), P(None, "tp"))
    return jax.shard_map(
        per_device, mesh=mesh, in_specs=in_specs, out_specs=out_specs, check_vma=False
    )
```

profile of v0, /device:TPU:0, one launch (start us, length us, event | category | flops | bytes accessed | tf_op | source)
XLA Modules:
  0.0 192.4 jit_solution(7465929102253558879)
XLA Ops:
  7.2 0.0 copy-start
  7.2 0.0 copy-start.1
  7.2 0.0 all-gather.5.cloned.1.call-start
  7.2 1.4 copy.44
  8.6 16.9 %all_to_all.38 = bf16[112,4,896]{2,0,1:T(8,128)(2,1)} all-to-all(bf16[112,4,896]{2,0,1:T(8,128)(2,1)S(1)} %bitcast.46), channel_id=1, replica_groups=mesh['rep'=8,'tp'=4] {'tp'}, dimensions={1} | all-to-all | bytes 1605632 | tf_op jit(solution)/shard_map/all_to_all | solution.py:32
  25.5 0.0 all-gather.5.cloned.1.call-update
  25.6 0.0 all-gather.3.cloned.1.call-start
  25.6 0.0 copy-start.2
  25.6 0.1 copy.43
  25.7 16.3 %all_to_all.39 = bf16[112,4,1152]{2,0,1:T(8,128)(2,1)} all-to-all(bf16[112,4,1152]{2,0,1:T(8,128)(2,1)S(1)} %bitcast.44), channel_id=1, replica_groups=mesh['rep'=8,'tp'=4] {'tp'}, dimensions={1} | all-to-all | bytes 2064384 | tf_op jit(solution)/shard_map/all_to_all | solution.py:31
  42.0 0.0 all-gather.3.cloned.1.call-update
  42.0 0.0 copy-start.3
  42.0 4.6 %convolution_convert_fusion = bf16[4,1152]{1,0:T(4,128)(2,1)S(1)} fusion(bf16[4,3584]{1,0:T(4,128)(2,1)S(1)} %copy-done.2, bf16[3584,1152]{1,0:T(8,128)(2,1)} %param.10), kind=kOutput, calls=%fused_computation | convolution fusion | flops 33034752 | bytes 8295424 | tf_op jit(solution)/shard_map/dot_general | solution.py:39
  46.7 7.6 %all_gather.9 = bf16[4,4608]{1,0:T(4,128)(2,1)S(1)} all-gather(bf16[4,1152]{1,0:T(4,128)(2,1)S(1)} %convolution_convert_fusion), channel_id=1, replica_groups=mesh['rep'=8,'tp'=4] {'tp'}, dimensions={1}, use_global_device_ids=true | all-gather | bytes 46080 | tf_op jit(solution)/shard_map/all_gather | solution.py:42
  54.4 0.1 multiply_cosine_fusion
  54.5 0.1 subtract_convert_fusion
  54.7 0.1 subtract_convert_fusion.1
  54.7 0.1 maximum_convert_fusion
  54.8 0.2 multiply_reduce_fusion
  55.0 0.1 broadcast_compare_fusion
  55.1 0.0 copy-done
  55.1 0.8 fusion.14
  55.9 9.1 %pmax.7 = f32[4,4,7]{2,1,0:T(4,128)S(1)} all-reduce(f32[4,4,7]{2,1,0:T(4,128)S(1)} %multiply_maximum_fusion), channel_id=1, replica_groups=mesh['rep'=8,'tp'=4] {'tp'}, use_global_device_ids=true, to_apply=%region_2.3 | all-reduce | flops 112 | bytes 896 | tf_op jit(solution)/shard_map/pmax | solution.py:71
  65.0 0.2 convert_reduce_fusion
  65.2 2.1 %fusion = f32[4,4,7,128]{3,2,1,0:T(8,128)S(1)} fusion(f32[4,4,7,512]{3,2,1,0:T(8,128)S(1)} %get-tuple-element.14, f32[4,4,7]{2,1,0:T(4,128)S(1)} %pmax.7, pred[4,512]{1,0:T(4,128)(4,1)S(1)} %broadcast_compare_fusion, bf16[4,512,512]{2,1,0:T(8,128)(2,1)} %param.13), kind=kOutput, calls=%fused_computation.1 | convolution fusion | flops 14852096 | bytes 2386368 | tf_op jit(solution)/shard_map/skgt,stkd->skgd/dot_general | solution.py:75
  67.3 16.0 %all-reduce = (f32[4,4,7,128]{3,2,1,0:T(8,128)S(1)}, f32[4,4,7]{2,1,0:T(4,128)S(1)}) all-reduce(f32[4,4,7,128]{3,2,1,0:T(8,128)S(1)} %fusion, f32[4,4,7]{2,1,0:T(4,128)S(1)} %convert_reduce_fusion), channel_id=1, replica_groups=mesh['rep'=8,'tp'=4] {'tp'}, use_global_device_ids=true, to_apply=%region_3.4 | all-reduce | flops 14448 | bytes 115584 | tf_op jit(solution)/shard_map/psum | solution.py:79
  83.3 0.1 divide_convert_fusion
  83.4 4.4 %convolution_convert_fusion.1 = bf16[4,896]{1,0:T(4,128)(2,1)} fusion(bf16[4,3584]{1,0:T(4,128)(2,1)S(1)} %convert_element_type.68, bf16[3584,896]{1,0:T(8,128)(2,1)} %param.11), kind=kOutput, calls=%fused_computation.9 | convolution fusion | flops 25693696 | bytes 6458368 | tf_op jit(solution)/shard_map/dot_general | solution.py:86
  87.8 3.1 %all-gather.5.cloned.1.call-done = bf16[3584,896]{1,0:T(8,128)(2,1)} async-done(((bf16[448,896]{1,0:T(8,128)(2,1)}), bf16[3584,896]{1,0:T(8,128)(2,1)}) %all-gather.5.cloned.1.call-update) | async-done | bytes 6422544 | tf_op jit(solution)/shard_map/all_gather | solution.py:36
  90.9 81.3 %all-gather.3.cloned.1.call-done = bf16[3584,1152]{1,0:T(8,128)(2,1)} async-done(((bf16[448,1152]{1,0:T(8,128)(2,1)}), bf16[3584,1152]{1,0:T(8,128)(2,1)}) %all-gather.3.cloned.1.call-update) | async-done | bytes 8257552 | tf_op jit(solution)/shard_map/all_gather | solution.py:35
  172.2 7.3 %copy.47 = bf16[3584,1152]{1,0:T(8,128)(2,1)} copy(bf16[3584,1152]{1,0:T(8,128)(2,1)} %all-gather.3.cloned.1.call-done) | data formatting | bytes 16515072
  179.5 6.1 %copy.48 = bf16[3584,896]{1,0:T(8,128)(2,1)} copy(bf16[3584,896]{1,0:T(8,128)(2,1)} %all-gather.5.cloned.1.call-done) | data formatting | bytes 12845056
  (20 shorter events, 0.2 us)
Async XLA Ops:
  7.2 47.9 %copy-start = (bf16[4,512,512]{2,1,0:T(8,128)(2,1)S(1)}, bf16[4,512,512]{2,1,0:T(8,128)(2,1)}, u32[]{:S(2)}) copy-start(bf16[4,512,512]{2,1,0:T(8,128)(2,1)} %param.12) | copy-start | bytes 6291460
  7.2 18.4 %copy-start.1 = (bf16[112,4608]{1,0:T(8,128)(2,1)S(1)}, bf16[112,4608]{1,0:T(8,128)(2,1)}, u32[]{:S(2)}) copy-start(bf16[112,4608]{1,0:T(8,128)(2,1)} %param.14) | copy-start | bytes 3096580
  7.2 83.7 %all-gather.5.cloned.1.call-start = ((), (), s32[]{:S(2)}) async-start(), calls=%async_computation.3 | async-start | bytes 7225344 | tf_op jit(solution)/shard_map/all_gather | solution.py:36
  25.6 146.6 %all-gather.3.cloned.1.call-start = ((), (), s32[]{:S(2)}) async-start(), calls=%async_computation.2 | async-start | bytes 9289728 | tf_op jit(solution)/shard_map/all_gather | solution.py:35
  25.6 16.4 %copy-start.2 = (bf16[4,3584]{1,0:T(4,128)(2,1)S(1)}, bf16[4,3584]{1,0:T(4,128)(2,1)}, u32[]{:S(2)}) copy-start(bf16[4,3584]{1,0:T(4,128)(2,1)} %param.8) | copy-start | bytes 86020
  42.0 12.2 %copy-start.3 = (s32[4]{0:T(128)S(1)}, s32[4]{0:T(128)}, u32[]{:S(2)}) copy-start(s32[4]{0:T(128)} %param.9) | copy-start | bytes 52
Sparse Core Ops, SparseCore 0:
  25.7 65.1 all-gather.4
  92.5 79.5 all-gather.2
where the time goes:
time: 193 us; the launch traced here: 192 us
  waiting for transfers between devices  84.4 us (44%)
  blocking collectives  65.8 us (34%)
  local copies, waits for them, and re-layouts  15 us (8%)
  between operations  14.2 us (7%)
  matrix products  11.9 us (6%)
    all_gather x1, waiting for transfers between devices, per_device(): lax.all_gather(pieces[0], 'rep', axis=0, tiled=True)  81.3 us
    all_to_all x1, blocking collectives, per_device(): lax.all_to_all(new_out, 'tp', split_axis=1, concat_axis=0, tiled=True)  16.9 us
    all_to_all x1, blocking collectives, per_device(): lax.all_to_all(new_qkv, 'tp', split_axis=1, concat_axis=0, tiled=True)  16.3 us
    psum x1, blocking collectives, per_device(): numerator, denominator = lax.psum((numer_part, denom_part), 'tp')  16 us
    unnamed x10, local copies, waits for them, and re-layouts  13.4 us
    pmax x1, blocking collectives, per_device(): top_score = lax.pmax(local_top, 'tp')  9.08 us
    all_gather x1, blocking collectives, per_device(): joined_rows = lax.all_gather(local_joined, 'tp', axis=1, tiled=True)  7.56 us
    dot_general x1, matrix products, per_device(): jnp.dot(hidden_state, old_qkv, preferred_element_type=jnp.float32)  4.65 us
  transfers between devices with their start and end apart: 2, of which 2 were waited for; matrix products, arithmetic and copies ran while one was open for 7% of the time, Pallas kernels for 0%

commit v1 on v0

--- a/solution.py
+++ b/solution.py
@@ -1,6 +1,10 @@
+import functools
+
 import jax
 import jax.numpy as jnp
 from jax import lax
+from jax.experimental import pallas as pl
+from jax.experimental.pallas import tpu as pltpu
 from jax.sharding import PartitionSpec as P
 
 HQ = 28
@@ -26,15 +30,7 @@
     )
 
 
-def per_device(hidden_state, lengths, old_qkv, old_out, cache_keys, cache_values, new_qkv, new_out):
-    pieces = (
-        lax.all_to_all(new_qkv, "tp", split_axis=1, concat_axis=0, tiled=True),
-        lax.all_to_all(new_out, "tp", split_axis=1, concat_axis=0, tiled=True),
-    )
-    qkv_tp, out_tp = (
-        lax.all_gather(pieces[0], "rep", axis=0, tiled=True),
-        lax.all_gather(pieces[1], "rep", axis=0, tiled=True),
-    )
+def per_device(hidden_state, lengths, old_qkv, old_out, cache_keys, cache_values):
     seq_count = hidden_state.shape[0]
     local_joined = jnp.dot(hidden_state, old_qkv, preferred_element_type=jnp.float32).astype(
         jnp.bfloat16
@@ -84,7 +80,162 @@
     denominator = denominator + own_weight
     attended = (numerator / denominator[..., None]).reshape(seq_count, q_width).astype(jnp.bfloat16)
     decoded = jnp.dot(attended, old_out, preferred_element_type=jnp.float32).astype(jnp.bfloat16)
-    return (decoded, qkv_tp, out_tp)
+    return decoded
+
+
+def native_move(new_qkv, new_out):
+    def move(block):
+        piece = lax.all_to_all(block, "tp", split_axis=1, concat_axis=0, tiled=True)
+        return lax.all_gather(piece, "rep", axis=0, tiled=True)
+
+    return move(new_qkv), move(new_out)
+
+
+def flip(index, bits, size):
+    out = index
+    bit = 1
+    while bit < size:
+        if (bits // bit) % 2:
+            out = out + bit - 2 * bit * ((index // bit) % 2)
+        bit *= 2
+    return out
+
+
+def move_kernel(reps, tps, qkv_ref, out_ref, qkv_full, out_full, *sems):
+    (a_send, a_recv, p_send, p_recv, m_send, m_recv, s_send, s_recv, own_sem) = sems
+    planes = reps // 2
+    rep, tp = lax.axis_index("rep"), lax.axis_index("tp")
+    plane, core = rep // 2, rep % 2
+    rows = qkv_ref.shape[0]
+    blocks, fulls = (qkv_ref, out_ref), (qkv_full, out_full)
+    widths = (qkv_full.shape[1], out_full.shape[1])
+    up = (lax.rem(plane + 1, planes) * 2 + core, tp)
+    down = (lax.rem(plane + planes - 1, planes) * 2 + core, tp)
+    twin = (plane * 2 + 1 - core, tp)
+    peers = [(rep, flip(tp, k, tps)) for k in range(1, tps)]
+
+    barrier = pltpu.get_barrier_semaphore()
+    partners = [up, down, twin] + peers
+    for device in partners:
+        pl.semaphore_signal(barrier, inc=1, device_id=device, device_id_type=pl.DeviceIdType.MESH)
+    pl.semaphore_wait(barrier, len(partners))
+
+    def rows_of(distance, k, w):
+        source = lax.rem(plane + planes - distance, planes) * 2 + core
+        start = (source * tps + flip(tp, k, tps)) * rows
+        return fulls[w].at[pl.ds(pl.multiple_of(start, rows), rows)]
+
+    def column(w, t):
+        start = pl.multiple_of(t * widths[w], 128)
+        return blocks[w].at[:, pl.ds(start, widths[w])]
+
+    def remote(source, target, send, recv, device):
+        copy = pltpu.make_async_remote_copy(
+            src_ref=source, dst_ref=target, send_sem=send, recv_sem=recv,
+            device_id=device, device_id_type=pl.DeviceIdType.MESH,
+        )
+        return copy
+
+    sent = []
+
+    def spread(distance, k, w, above, below, source=None):
+        target = rows_of(distance, k, w)
+        source = target if source is None else source
+        if above:
+            hop = distance % planes
+            copy = remote(source, target, p_send.at[hop, k, w], p_recv.at[hop, k, w], up)
+            copy.start()
+            sent.append(copy)
+        if below:
+            hop = (planes - distance) % planes
+            copy = remote(source, target, m_send.at[hop, k, w], m_recv.at[hop, k, w], down)
+            copy.start()
+            sent.append(copy)
+        copy = remote(source, target, s_send.at[distance, k, w], s_recv.at[distance, k, w], twin)
+        copy.start()
+        sent.append(copy)
+
+    def arrived_up(hop, k, w):
+        target = rows_of(hop + 1, k, w)
+        remote(target, target, p_send.at[hop, k, w], p_recv.at[hop, k, w], up).wait_recv()
+
+    def arrived_down(hop, k, w):
+        target = rows_of(planes - hop - 1, k, w)
+        remote(target, target, m_send.at[hop, k, w], m_recv.at[hop, k, w], down).wait_recv()
+
+    local = []
+    for k in range(1, tps):
+        for w in range(2):
+            copy = remote(
+                column(w, flip(tp, k, tps)), rows_of(0, 0, w),
+                a_send.at[k, w], a_recv.at[k, w], peers[k - 1],
+            )
+            copy.start()
+            sent.append(copy)
+    for w in range(2):
+        spread(0, 0, w, True, True, column(w, tp))
+        copy = pltpu.make_async_copy(column(w, tp), rows_of(0, 0, w), own_sem.at[w])
+        copy.start()
+        local.append(copy)
+    for k in range(1, tps):
+        for w in range(2):
+            target = rows_of(0, k, w)
+            remote(target, target, a_send.at[k, w], a_recv.at[k, w], peers[k - 1]).wait_recv()
+            spread(0, k, w, True, True)
+
+    half = planes // 2
+    for distance in range(1, half):
+        for k in range(tps):
+            for w in range(2):
+                last = distance + 1 == half
+                arrived_up(distance - 1, k, w)
+                spread(distance, k, w, not last or k < tps // 2, False)
+                arrived_down(distance - 1, k, w)
+                spread(planes - distance, k, w, False, not last or k >= tps // 2)
+    for k in range(tps // 2):
+        for w in range(2):
+            arrived_up(half - 1, k, w)
+            spread(half, k, w, False, False)
+            other = k + tps // 2
+            arrived_down(half - 1, other, w)
+            spread(half, other, w, False, False)
+
+    for distance in range(planes):
+        for k in range(tps):
+            for w in range(2):
+                source = lax.rem(plane + planes - distance, planes) * 2 + 1 - core
+                start = (source * tps + flip(tp, k, tps)) * rows
+                target = fulls[w].at[pl.ds(pl.multiple_of(start, rows), rows)]
+                remote(
+                    target, target, s_send.at[distance, k, w], s_recv.at[distance, k, w], twin
+                ).wait_recv()
+    for copy in sent:
+        copy.wait_send()
+    for copy in local:
+        copy.wait()
+
+
+def move(mesh, new_qkv, new_out):
+    reps, tps = mesh.shape["rep"], mesh.shape["tp"]
+    rows = new_qkv.shape[0]
+    widths = (new_qkv.shape[1] // tps, new_out.shape[1] // tps)
+    tiled = rows % 16 == 0 and all(width % 128 == 0 for width in widths)
+    if reps % 4 or not tiled:
+        return native_move(new_qkv, new_out)
+    planes = reps // 2
+    sem = pltpu.SemaphoreType.DMA
+    return pl.pallas_call(
+        functools.partial(move_kernel, reps, tps),
+        out_shape=[
+            jax.ShapeDtypeStruct((rows * reps * tps, width), new_qkv.dtype) for width in widths
+        ],
+        in_specs=[pl.BlockSpec(memory_space=pl.ANY)] * 2,
+        out_specs=[pl.BlockSpec(memory_space=pl.ANY)] * 2,
+        scratch_shapes=[sem((tps, 2)), sem((tps, 2))]
+        + [sem((planes // 2, tps, 2)) for _ in range(4)]
+        + [sem((planes, tps, 2)), sem((planes, tps, 2)), sem((2,))],
+        compiler_params=pltpu.CompilerParams(collective_id=0, has_side_effects=True),
+    )(new_qkv, new_out)
 
 
 def solution(mesh):
@@ -99,6 +250,11 @@
         P(("rep", "tp"), None),
     )
     out_specs = (P("rep", "tp"), P(None, "tp"), P(None, "tp"))
+
+    def step(*args):
+        decoded = per_device(*args[:6])
+        return (decoded, *move(mesh, *args[6:]))
+
     return jax.shard_map(
-        per_device, mesh=mesh, in_specs=in_specs, out_specs=out_specs, check_vma=False
-    )
+        step, mesh=mesh, in_specs=in_specs, out_specs=out_specs, check_vma=False
+    )

time: 193 us -> 188 us (0.974)
  Pallas kernels: 0 us -> 124 us
  waiting for transfers between devices: 84.4 us -> 0 us
  blocking collectives: 65.8 us -> 35.2 us
  between operations: 14.2 us -> 0.77 us
    pallas_call x0 -> x1, Pallas kernels: none -> 124 us  [move(): pl.pallas_call(functools.partial(move_kernel, reps, tps), out_shape=[jax....]
    all_gather x2 -> x0, waiting for transfers between devices: 84.4 us -> none  [the longest x1 81.3 us: per_device(): lax.all_gather(pieces[0], 'rep', axis=0, tiled=True)]
    all_to_all x2 -> x0, blocking collectives: 33.2 us -> none  [the longest x1 16.9 us: per_device(): lax.all_to_all(new_out, 'tp', split_axis=1, concat_axis=0, tiled=True)]
    all_gather x1, blocking collectives: 7.56 us -> 9.71 us  [per_device(): joined_rows = lax.all_gather(local_joined, 'tp', axis=1, tiled=True)]
    unnamed x10 -> x4, local copies, waits for them, and re-layouts: 13.4 us -> 13.4 us
  transfers between devices with their start and end apart: 2 -> 0, of which waited for: 2 -> 0; matrix products, arithmetic and copies ran while one was open for 7% -> 0% of each run, Pallas kernels for 0% -> 0%
where the time goes in v1:
time: 188 us
  Pallas kernels  124 us (66%)
  blocking collectives  35.2 us (19%)
  local copies, waits for them, and re-layouts  13.6 us (7%)
  matrix products  11.7 us (6%)
  other arithmetic  2.43 us (1%)
    pallas_call x1, Pallas kernels, move(): pl.pallas_call(functools.partial(move_kernel, reps, tps), out_shape=[jax....  124 us
    psum x1, blocking collectives, per_device(): numerator, denominator = lax.psum((numer_part, denom_part), 'tp')  16.4 us
    unnamed x4, local copies, waits for them, and re-layouts  13.4 us
    all_gather x1, blocking collectives, per_device(): joined_rows = lax.all_gather(local_joined, 'tp', axis=1, tiled=True)  9.71 us
    pmax x1, blocking collectives, per_device(): top_score = lax.pmax(local_top, 'tp')  9.11 us
    dot_general x1, matrix products, per_device(): jnp.dot(hidden_state, old_qkv, preferred_element_type=jnp.float32)  4.53 us
    dot_general x1, matrix products, per_device(): jnp.dot(attended, old_out, preferred_element_type=jnp.float32)  4.38 us

profile of v1, /device:TPU:0, one launch (start us, length us, event | category | flops | bytes accessed | tf_op | source)
XLA Modules:
  0.0 187.7 jit_solution(2732361818515003150)
XLA Ops:
  0.6 0.0 copy-start
  0.6 0.8 convert_element_type.58
  1.5 0.7 broadcast_compare_fusion
  2.2 0.1 multiply_cosine_fusion
  2.3 4.5 %convolution_convert_fusion = bf16[4,1152]{1,0:T(4,128)(2,1)S(1)} fusion(bf16[4,3584]{1,0:T(4,128)(2,1)} %param.8, bf16[3584,1152]{1,0:T(8,128)(2,1)} %param.10), kind=kOutput, calls=%fused_computation | convolution fusion | flops 33034752 | bytes 8295424 | tf_op jit(solution)/shard_map/dot_general | solution.py:35
  6.8 9.7 %all_gather.3 = bf16[4,4608]{1,0:T(4,128)(2,1)S(1)} all-gather(bf16[4,1152]{1,0:T(4,128)(2,1)S(1)} %convolution_convert_fusion), channel_id=1, replica_groups=mesh['rep'=8,'tp'=4] {'tp'}, dimensions={1}, use_global_device_ids=true | all-gather | bytes 46080 | tf_op jit(solution)/shard_map/all_gather | solution.py:38
  16.6 0.1 subtract_convert_fusion.1
  16.7 0.1 maximum_convert_fusion
  16.8 0.1 subtract_convert_fusion
  17.0 0.2 multiply_reduce_fusion
  17.2 0.0 copy-done
  17.2 0.8 fusion.14
  18.0 9.1 %pmax.7 = f32[4,4,7]{2,1,0:T(4,128)S(1)} all-reduce(f32[4,4,7]{2,1,0:T(4,128)S(1)} %multiply_maximum_fusion), channel_id=1, replica_groups=mesh['rep'=8,'tp'=4] {'tp'}, use_global_device_ids=true, to_apply=%region_2.3 | all-reduce | flops 112 | bytes 896 | tf_op jit(solution)/shard_map/pmax | solution.py:67
  27.1 0.2 convert_reduce_fusion
  27.3 2.0 %fusion = f32[4,4,7,128]{3,2,1,0:T(8,128)S(1)} fusion(f32[4,4,7,512]{3,2,1,0:T(8,128)S(1)} %get-tuple-element.18, f32[4,4,7]{2,1,0:T(4,128)S(1)} %pmax.7, pred[4,512]{1,0:T(4,128)(4,1)S(1)} %broadcast_compare_fusion, bf16[4,512,512]{2,1,0:T(8,128)(2,1)} %param.13), kind=kOutput, calls=%fused_computation.1 | convolution fusion | flops 14852096 | bytes 2386368 | tf_op jit(solution)/shard_map/skgt,stkd->skgd/dot_general | solution.py:71
  29.3 16.4 %all-reduce = (f32[4,4,7,128]{3,2,1,0:T(8,128)S(1)}, f32[4,4,7]{2,1,0:T(4,128)S(1)}) all-reduce(f32[4,4,7,128]{3,2,1,0:T(8,128)S(1)} %fusion, f32[4,4,7]{2,1,0:T(4,128)S(1)} %convert_reduce_fusion), channel_id=1, replica_groups=mesh['rep'=8,'tp'=4] {'tp'}, use_global_device_ids=true, to_apply=%region_3.4 | all-reduce | flops 14448 | bytes 115584 | tf_op jit(solution)/shard_map/psum | solution.py:75
  45.8 0.1 divide_convert_fusion
  45.9 4.4 %convolution_convert_fusion.1 = bf16[4,896]{1,0:T(4,128)(2,1)} fusion(bf16[4,3584]{1,0:T(4,128)(2,1)S(1)} %convert_element_type.68, bf16[3584,896]{1,0:T(8,128)(2,1)} %param.11), kind=kOutput, calls=%fused_computation.9 | convolution fusion | flops 25693696 | bytes 6458368 | tf_op jit(solution)/shard_map/dot_general | solution.py:82
  50.3 124.0 %shard_map.103 = (bf16[3584,1152]{1,0:T(8,128)(2,1)}, bf16[3584,896]{1,0:T(8,128)(2,1)}) custom-call(bf16[112,4608]{1,0:T(8,128)(2,1)} %qkv_ref.1, bf16[112,3584]{1,0:T(8,128)(2,1)} %out_ref.1), custom_call_target="tpu_custom_call" | custom-call | tf_op jit(solution)/shard_map/pallas_call | solution.py:227
  174.3 7.3 %copy.37 = bf16[3584,1152]{1,0:T(8,128)(2,1)} copy(bf16[3584,1152]{1,0:T(8,128)(2,1)} %get-tuple-element.23) | data formatting | bytes 16515072
  181.6 6.1 %copy.38 = bf16[3584,896]{1,0:T(8,128)(2,1)} copy(bf16[3584,896]{1,0:T(8,128)(2,1)} %get-tuple-element.24) | data formatting | bytes 12845056
  (16 shorter events, 0.2 us)
Async XLA Ops:
  0.6 16.5 %copy-start = (bf16[4,512,512]{2,1,0:T(8,128)(2,1)S(1)}, bf16[4,512,512]{2,1,0:T(8,128)(2,1)}, u32[]{:S(2)}) copy-start(bf16[4,512,512]{2,1,0:T(8,128)(2,1)} %param.12) | copy-start | bytes 6291460

commit v2 on v0

--- a/solution.py
+++ b/solution.py
@@ -1,11 +1,19 @@
+import functools
+
 import jax
 import jax.numpy as jnp
 from jax import lax
+from jax.experimental import pallas as pl
+from jax.experimental.pallas import tpu as pltpu
 from jax.sharding import PartitionSpec as P
 
 HQ = 28
 KVH = 4
 HD = 128
+PAD = 8
+VMEM_BYTES = 67043328
+SLACK = 600000
+MESH = pl.DeviceIdType.MESH
 
 
 ROPE_BASE = 1000000.0
@@ -26,15 +34,7 @@
     )
 
 
-def per_device(hidden_state, lengths, old_qkv, old_out, cache_keys, cache_values, new_qkv, new_out):
-    pieces = (
-        lax.all_to_all(new_qkv, "tp", split_axis=1, concat_axis=0, tiled=True),
-        lax.all_to_all(new_out, "tp", split_axis=1, concat_axis=0, tiled=True),
-    )
-    qkv_tp, out_tp = (
-        lax.all_gather(pieces[0], "rep", axis=0, tiled=True),
-        lax.all_gather(pieces[1], "rep", axis=0, tiled=True),
-    )
+def per_device(hidden_state, lengths, old_qkv, old_out, cache_keys, cache_values):
     seq_count = hidden_state.shape[0]
     local_joined = jnp.dot(hidden_state, old_qkv, preferred_element_type=jnp.float32).astype(
         jnp.bfloat16
@@ -84,7 +84,366 @@
     denominator = denominator + own_weight
     attended = (numerator / denominator[..., None]).reshape(seq_count, q_width).astype(jnp.bfloat16)
     decoded = jnp.dot(attended, old_out, preferred_element_type=jnp.float32).astype(jnp.bfloat16)
-    return (decoded, qkv_tp, out_tp)
+    return decoded
+
+
+def native_move(new_qkv, new_out):
+    def move(block):
+        piece = lax.all_to_all(block, "tp", split_axis=1, concat_axis=0, tiled=True)
+        return lax.all_gather(piece, "rep", axis=0, tiled=True)
+
+    return move(new_qkv), move(new_out)
+
+
+def flip(index, bits, size):
+    out = index
+    bit = 1
+    while bit < size:
+        if (bits // bit) % 2:
+            out = out + bit - 2 * bit * ((index // bit) % 2)
+        bit *= 2
+    return out
+
+
+def step_kernel(
+    planes, tps,
+    hidden, cosine, sine, live, old_qkv, old_out, keys, values, new_qkv, new_out,
+    decoded, qkv_full, out_full,
+    a_send, a_recv, u_send, u_recv, d_send, d_recv, s_send, s_recv, own_sem, load_sem,
+    j_send, j_recv, n_send, n_recv,
+    w_qkv, w_out, k_held, v_held, joined, rotated, own_score, own_value, parts, attended,
+):
+    rep, tp = lax.axis_index("rep"), lax.axis_index("tp")
+    plane, core = rep // 2, rep % 2
+    rows = new_qkv.shape[0]
+    blocks, fulls = (new_qkv, new_out), (qkv_full, out_full)
+    widths = (qkv_full.shape[1], out_full.shape[1])
+    up = (jnp.minimum(plane + 1, planes - 1) * 2 + core, tp)
+    down = (jnp.maximum(plane - 1, 0) * 2 + core, tp)
+    twin = (plane * 2 + 1 - core, tp)
+    peers = [(rep, flip(tp, k, tps)) for k in range(1, tps)]
+    can_up, can_down = plane < planes - 1, plane > 0
+
+    barrier = pltpu.get_barrier_semaphore()
+    for device in [twin] + peers:
+        pl.semaphore_signal(barrier, inc=1, device_id=device, device_id_type=MESH)
+
+    @pl.when(can_up)
+    def _():
+        pl.semaphore_signal(barrier, inc=1, device_id=up, device_id_type=MESH)
+
+    @pl.when(can_down)
+    def _():
+        pl.semaphore_signal(barrier, inc=1, device_id=down, device_id_type=MESH)
+
+    @pl.when(can_up & can_down)
+    def _():
+        pl.semaphore_wait(barrier, tps + 2)
+
+    @pl.when(jnp.logical_not(can_up & can_down))
+    def _():
+        pl.semaphore_wait(barrier, tps + 1)
+
+    def remote(source, target, send, recv, device):
+        return pltpu.make_async_remote_copy(
+            src_ref=source, dst_ref=target, send_sem=send, recv_sem=recv,
+            device_id=device, device_id_type=MESH,
+        )
+
+    def rows_of(source_plane, source_core, k, w):
+        start = ((source_plane * 2 + source_core) * tps + flip(tp, k, tps)) * rows
+        return fulls[w].at[pl.ds(pl.multiple_of(start, rows), rows)]
+
+    def column(w, t):
+        return blocks[w].at[:, pl.ds(pl.multiple_of(t * widths[w], 128), widths[w])]
+
+    def in_plane(k, w):
+        return remote(
+            column(w, flip(tp, k, tps)), rows_of(plane, core, 0, w),
+            a_send.at[k, w], a_recv.at[k, w], peers[k - 1],
+        )
+
+    def piece(d, k, w):
+        target = rows_of(plane - d, core, k, w)
+        return target, (column(w, tp) if d == 0 and k == 0 else target)
+
+    def to_up(d, k, w):
+        target, source = piece(d, k, w)
+        return remote(source, target, u_send.at[d, k, w], u_recv.at[d, k, w], up)
+
+    def to_down(d, k, w):
+        target, source = piece(-d, k, w)
+        return remote(source, target, d_send.at[d, k, w], d_recv.at[d, k, w], down)
+
+    def to_twin(d, k, w):
+        target, source = piece(d, k, w)
+        slot = d + planes - 1
+        return remote(source, target, s_send.at[slot, k, w], s_recv.at[slot, k, w], twin)
+
+    def own(k, w):
+        @pl.when(can_up)
+        def _():
+            to_up(0, k, w).start()
+
+        @pl.when(can_down)
+        def _():
+            to_down(0, k, w).start()
+
+        to_twin(0, k, w).start()
+
+    def relay(d):
+        for k in range(tps):
+            for w in range(2):
+
+                @pl.when(plane >= d)
+                def _():
+                    target = rows_of(plane - d, core, k, w)
+                    remote(
+                        target, target, u_send.at[d - 1, k, w], u_recv.at[d - 1, k, w], up
+                    ).wait_recv()
+
+                    @pl.when(can_up)
+                    def _():
+                        to_up(d, k, w).start()
+
+                    to_twin(d, k, w).start()
+
+                @pl.when(plane + d < planes)
+                def _():
+                    target = rows_of(plane + d, core, k, w)
+                    remote(
+                        target, target, d_send.at[d - 1, k, w], d_recv.at[d - 1, k, w], down
+                    ).wait_recv()
+
+                    @pl.when(can_down)
+                    def _():
+                        to_down(d, k, w).start()
+
+                    to_twin(-d, k, w).start()
+
+    for k in range(1, tps):
+        for w in range(2):
+            in_plane(k, w).start()
+    for w in range(2):
+        own(0, w)
+    locals_ = [
+        pltpu.make_async_copy(column(w, tp), rows_of(plane, core, 0, w), own_sem.at[w])
+        for w in range(2)
+    ]
+    loads = [
+        pltpu.make_async_copy(source, target, load_sem.at[i])
+        for i, (source, target) in enumerate(
+            ((old_qkv, w_qkv), (keys, k_held), (values, v_held), (old_out, w_out))
+        )
+    ]
+    for copy in locals_ + loads:
+        copy.start()
+    for k in range(1, tps):
+        for w in range(2):
+            target = rows_of(plane, core, k, w)
+            remote(
+                target, target, a_send.at[k, w], a_recv.at[k, w], peers[k - 1]
+            ).wait_recv()
+            own(k, w)
+
+    seqs = hidden.shape[0]
+    tile = 128
+    loads[0].wait()
+
+    @pl.loop(0, w_qkv.shape[1] // tile)
+    def _(i):
+        at = pl.ds(pl.multiple_of(i * tile, tile), tile)
+        joined[tp, :, at] = jnp.dot(
+            hidden[...], w_qkv[:, at], preferred_element_type=jnp.float32
+        ).astype(joined.dtype)
+
+    def send_joined(k):
+        return remote(
+            joined.at[tp], joined.at[tp], j_send.at[k], j_recv.at[k], peers[k - 1]
+        )
+
+    for k in range(1, tps):
+        send_joined(k).start()
+
+    relay(1)
+
+    for k in range(1, tps):
+        slot = joined.at[flip(tp, k, tps)]
+        remote(slot, slot, j_send.at[k], j_recv.at[k], peers[k - 1]).wait_recv()
+    for copy in loads[1:]:
+        copy.wait()
+
+    group = HQ // KVH
+    per_slot = joined.shape[2] // HD
+    inv_root = 1.0 / jnp.sqrt(jnp.float32(HD))
+
+    def head(j):
+        at = (j % per_slot) * HD
+        return joined[j // per_slot, :, at : at + HD].astype(jnp.float32)
+
+    def turn(v):
+        swapped = jnp.concatenate([v[:, HD // 2 :], v[:, : HD // 2]], axis=1)
+        return (v * cosine[...] + swapped * sine[...]).astype(jnp.bfloat16).astype(jnp.float32)
+
+    rotated[...] = jnp.zeros_like(rotated)
+    own_score[...] = jnp.zeros_like(own_score)
+    own_value[...] = jnp.zeros_like(own_value)
+    for kv in range(KVH):
+        own_key = turn(head(HQ + kv))
+        new_value = head(HQ + KVH + kv)
+        for g in range(group):
+            query = turn(head(kv * group + g))
+            rotated[:, kv * PAD + g, :] = query
+            score = jnp.sum(query * own_key, axis=1, keepdims=True) * inv_root
+            own_score[:, kv * PAD + g, :] = jnp.broadcast_to(score, (seqs, HD))
+            own_value[:, kv * PAD + g, :] = new_value
+
+    @pl.loop(0, seqs)
+    def _(s):
+        is_live = live[pl.ds(s, 1), :] > 0.0
+        for kv in range(KVH):
+            at = slice(kv * HD, (kv + 1) * HD)
+            lanes = slice(kv * PAD, (kv + 1) * PAD)
+            query = rotated[s, lanes, :].astype(jnp.bfloat16)
+            scores = lax.dot_general(
+                query, k_held[s, :, at], (((1,), (1,)), ((), ())),
+                preferred_element_type=jnp.float32,
+            ) * inv_root
+            scores = jnp.where(is_live, scores, jnp.float32(-1e30))
+            top = jnp.max(scores, axis=1, keepdims=True)
+            weights = jnp.where(is_live, jnp.exp(scores - top), 0.0).astype(jnp.bfloat16)
+            total = jnp.sum(weights.astype(jnp.float32), axis=1, keepdims=True)
+            parts[tp, 0, s, lanes, :] = jnp.dot(
+                weights, v_held[s, :, at], preferred_element_type=jnp.float32
+            )
+            parts[tp, 1, s, lanes, :] = jnp.broadcast_to(top, (PAD, HD))
+            parts[tp, 2, s, lanes, :] = jnp.broadcast_to(total, (PAD, HD))
+
+    def send_parts(k):
+        return remote(parts.at[tp], parts.at[tp], n_send.at[k], n_recv.at[k], peers[k - 1])
+
+    for k in range(1, tps):
+        send_parts(k).start()
+
+    for d in range(2, planes - 1):
+        relay(d)
+
+    for k in range(1, tps):
+        slot = parts.at[flip(tp, k, tps)]
+        remote(slot, slot, n_send.at[k], n_recv.at[k], peers[k - 1]).wait_recv()
+
+    @pl.loop(0, seqs)
+    def _(s):
+        mine = own_score[s]
+        top = mine
+        for t in range(tps):
+            top = jnp.maximum(top, parts[t, 1, s])
+        mine = jnp.exp(mine - top).astype(jnp.bfloat16).astype(jnp.float32)
+        numerator, denominator = mine * own_value[s], mine
+        for t in range(tps):
+            scale = jnp.exp(parts[t, 1, s] - top)
+            numerator = numerator + parts[t, 0, s] * scale
+            denominator = denominator + parts[t, 2, s] * scale
+        rotated[s] = numerator / denominator
+
+    for j in range(HQ):
+        row = (j // group) * PAD + j % group
+        attended[:, j * HD : (j + 1) * HD] = rotated[:, row, :].astype(attended.dtype)
+
+    @pl.loop(0, w_out.shape[1] // tile)
+    def _(i):
+        at = pl.ds(pl.multiple_of(i * tile, tile), tile)
+        decoded[:, at] = jnp.dot(
+            attended[...], w_out[:, at], preferred_element_type=jnp.float32
+        ).astype(decoded.dtype)
+
+    relay(planes - 1)
+
+    for d in range(planes):
+        for k in range(tps):
+            for w in range(2):
+
+                def from_twin(e):
+                    target = rows_of(plane - e, 1 - core, k, w)
+                    slot = e + planes - 1
+                    return remote(
+                        target, target, s_send.at[slot, k, w], s_recv.at[slot, k, w], twin
+                    )
+
+                @pl.when(plane >= d)
+                def _():
+                    from_twin(d).wait_recv()
+                    to_twin(d, k, w).wait_send()
+
+                    @pl.when(can_up)
+                    def _():
+                        to_up(d, k, w).wait_send()
+
+                if d:
+
+                    @pl.when(plane + d < planes)
+                    def _():
+                        from_twin(-d).wait_recv()
+                        to_twin(-d, k, w).wait_send()
+
+                @pl.when((plane + d < planes) & can_down)
+                def _():
+                    to_down(d, k, w).wait_send()
+
+    for k in range(1, tps):
+        for w in range(2):
+            in_plane(k, w).wait_send()
+        send_joined(k).wait_send()
+        send_parts(k).wait_send()
+    for copy in locals_:
+        copy.wait()
+
+
+def fused(mesh, hidden, lengths, old_qkv, old_out, keys, values, new_qkv, new_out):
+    reps, tps = mesh.shape["rep"], mesh.shape["tp"]
+    planes = reps // 2
+    seqs, positions = keys.shape[:2]
+    rows = new_qkv.shape[0]
+    widths = (new_qkv.shape[1] // tps, new_out.shape[1] // tps)
+    half = HD // 2
+    frequency = ROPE_BASE ** (-2.0 * jnp.arange(half, dtype=jnp.float32) / (2 * half))
+    angles = lengths.astype(jnp.float32)[:, None] * frequency
+    cosine, sine = jnp.cos(angles), jnp.sin(angles)
+    cosine = jnp.concatenate([cosine, cosine], axis=1)
+    sine = jnp.concatenate([-sine, sine], axis=1)
+    places = lax.axis_index("tp") * positions + jnp.arange(positions, dtype=jnp.int32)
+    live = (places[None, :] < lengths[:, None]).astype(jnp.float32)
+
+    sem = pltpu.SemaphoreType.DMA
+    whole, anywhere = pl.BlockSpec(memory_space=pltpu.VMEM), pl.BlockSpec(memory_space=pl.ANY)
+    in_hbm = pl.BlockSpec(memory_space=pltpu.HBM)
+    f32, bf16 = jnp.float32, jnp.bfloat16
+    padded = KVH * PAD
+    landed = 2 * rows * reps * tps * sum(widths)
+    scratch = [sem((tps, 2)), sem((tps, 2))]
+    scratch += [sem((planes, tps, 2)) for _ in range(4)]
+    scratch += [sem((2 * planes - 1, tps, 2)) for _ in range(2)]
+    scratch += [sem((2,)), sem((4,))] + [sem((tps,)) for _ in range(4)]
+    scratch += [pltpu.VMEM(x.shape, x.dtype) for x in (old_qkv, old_out, keys, values)]
+    scratch += [
+        pltpu.VMEM((tps, seqs, widths[0]), bf16),
+        pltpu.VMEM((seqs, padded, HD), f32),
+        pltpu.VMEM((seqs, padded, HD), f32),
+        pltpu.VMEM((seqs, padded, HD), f32),
+        pltpu.VMEM((tps, 3, seqs, padded, HD), f32),
+        pltpu.VMEM((seqs, HQ * HD), bf16),
+    ]
+    return pl.pallas_call(
+        functools.partial(step_kernel, planes, tps),
+        out_shape=[jax.ShapeDtypeStruct((seqs, widths[1]), bf16)]
+        + [pltpu.VMEM((rows * reps * tps, width), bf16) for width in widths],
+        in_specs=[whole] * 4 + [in_hbm] * 6,
+        out_specs=[whole] + [anywhere] * 2,
+        scratch_shapes=scratch,
+        compiler_params=pltpu.CompilerParams(
+            collective_id=0, has_side_effects=True, vmem_limit_bytes=VMEM_BYTES - landed - SLACK
+        ),
+    )(hidden, cosine, sine, live, old_qkv, old_out, keys, values, new_qkv, new_out)
 
 
 def solution(mesh):
@@ -99,6 +458,15 @@
         P(("rep", "tp"), None),
     )
     out_specs = (P("rep", "tp"), P(None, "tp"), P(None, "tp"))
+
+    def step(*args):
+        reps, tps = mesh.shape["rep"], mesh.shape["tp"]
+        widths = [x.shape[1] // tps for x in args[6:]]
+        tiled = args[6].shape[0] % 16 == 0 and all(width % 128 == 0 for width in widths)
+        if reps % 4 or not tiled:
+            return (per_device(*args[:6]), *native_move(*args[6:]))
+        return tuple(fused(mesh, *args))
+
     return jax.shard_map(
-        per_device, mesh=mesh, in_specs=in_specs, out_specs=out_specs, check_vma=False
-    )
+        step, mesh=mesh, in_specs=in_specs, out_specs=out_specs, check_vma=False
+    )

time: 193 us -> 139 us (0.72)
  Pallas kernels: 0 us -> 129 us
  waiting for transfers between devices: 84.4 us -> 0 us
  blocking collectives: 65.8 us -> 0 us
  between operations: 14.2 us -> 0.65 us
  matrix products: 11.9 us -> 0 us
  local copies, waits for them, and re-layouts: 15 us -> 6.7 us
    pallas_call x0 -> x1, Pallas kernels: none -> 129 us  [fused(): pl.pallas_call(functools.partial(step_kernel, planes, tps), out_shape=[ja...]
    all_gather x2 -> x0, waiting for transfers between devices: 84.4 us -> none  [the longest x1 81.3 us: per_device(): lax.all_gather(pieces[0], 'rep', axis=0, tiled=True)]
    all_to_all x2 -> x0, blocking collectives: 33.2 us -> none  [the longest x1 16.9 us: per_device(): lax.all_to_all(new_out, 'tp', split_axis=1, concat_axis=0, tiled=True)]
    psum x1 -> x0, blocking collectives: 16 us -> none  [per_device(): numerator, denominator = lax.psum((numer_part, denom_part), 'tp')]
    dot_general x4 -> x0, matrix products: 11.9 us -> none  [the longest x1 4.65 us: per_device(): jnp.dot(hidden_state, old_qkv, preferred_element_type=jnp.float32)]
    pmax x1 -> x0, blocking collectives: 9.08 us -> none  [per_device(): top_score = lax.pmax(local_top, 'tp')]
    all_gather x1 -> x0, blocking collectives: 7.56 us -> none  [per_device(): joined_rows = lax.all_gather(local_joined, 'tp', axis=1, tiled=True)]
    unnamed x10 -> x5, local copies, waits for them, and re-layouts: 13.4 us -> 6.7 us
  transfers between devices with their start and end apart: 2 -> 0, of which waited for: 2 -> 0; matrix products, arithmetic and copies ran while one was open for 7% -> 0% of each run, Pallas kernels for 0% -> 0%
where the time goes in v2:
time: 139 us
  Pallas kernels  129 us (93%)
  local copies, waits for them, and re-layouts  6.7 us (5%)
  other arithmetic  2.77 us (2%)
    pallas_call x1, Pallas kernels, fused(): pl.pallas_call(functools.partial(step_kernel, planes, tps), out_shape=[ja...  129 us
    unnamed x5, local copies, waits for them, and re-layouts  6.7 us

profile of v2, /device:TPU:0, one launch (start us, length us, event | category | flops | bytes accessed | tf_op | source)
XLA Modules:
  0.0 139.2 jit_solution(9115144974544376772)
XLA Ops:
  0.6 0.7 convert_element_type.6
  1.3 0.1 fusion
  1.4 0.7 pad_maximum_fusion
  2.1 1.3 compare_convert_fusion.live
  3.4 129.1 %shard_map.103 = (bf16[4,896]{1,0:T(4,128)(2,1)}, bf16[3584,1152]{1,0:T(8,128)(2,1)S(1)}, bf16[3584,896]{1,0:T(8,128)(2,1)S(1)}) custom-call(bf16[4,3584]{1,0:T(4,128)(2,1)} %hidden.1, f32[4,128]{1,0:T(4,128)} %get-tuple-element.6.cosine, f32[4,128]{1,0:T(4,128)} %get-tuple-element.7.sine, f32[4,512]{1,0:T(4,128)} %compare_convert_fusion.live, ...), custom_call_target="tpu_custom_call" | custom-call | tf_op jit(solution)/shard_map/pallas_call | solution.py:436
  132.5 2.7 %copy.15 = bf16[3584,896]{1,0:T(8,128)(2,1)} copy(bf16[3584,896]{1,0:T(8,128)(2,1)S(1)} %get-tuple-element.10) | data formatting | bytes 12845056
  135.2 0.0 copy-start
  135.2 3.3 %copy.14 = bf16[3584,1152]{1,0:T(8,128)(2,1)} copy(bf16[3584,1152]{1,0:T(8,128)(2,1)S(1)} %get-tuple-element.9) | data formatting | bytes 16515072
  138.6 0.0 copy-done
  138.6 0.6 copy.16
  (2 shorter events, 0.0 us)
Async XLA Ops:
  135.2 3.4 %copy-start = (bf16[4,896]{1,0:T(4,128)(2,1)S(1)}, bf16[4,896]{1,0:T(4,128)(2,1)}, u32[]{:S(2)}) copy-start(bf16[4,896]{1,0:T(4,128)(2,1)} %get-tuple-element.14) | copy-start | bytes 21508

commit v3 on v2

--- a/solution.py
+++ b/solution.py
@@ -2,6 +2,7 @@
 
 import jax
 import jax.numpy as jnp
+import numpy as np
 from jax import lax
 from jax.experimental import pallas as pl
 from jax.experimental.pallas import tpu as pltpu
@@ -11,6 +12,7 @@
 KVH = 4
 HD = 128
 PAD = 8
+CUTS = 8
 VMEM_BYTES = 67043328
 SLACK = 600000
 MESH = pl.DeviceIdType.MESH
@@ -107,11 +109,12 @@
 
 def step_kernel(
     planes, tps,
-    hidden, cosine, sine, live, old_qkv, old_out, keys, values, new_qkv, new_out,
+    hidden, lengths, frequency, old_qkv, old_out, keys, values, new_qkv, new_out,
     decoded, qkv_full, out_full,
     a_send, a_recv, u_send, u_recv, d_send, d_recv, s_send, s_recv, own_sem, load_sem,
     j_send, j_recv, n_send, n_recv,
     w_qkv, w_out, k_held, v_held, joined, rotated, own_score, own_value, parts, attended,
+    cosine, sine,
 ):
     rep, tp = lax.axis_index("rep"), lax.axis_index("tp")
     plane, core = rep // 2, rep % 2
@@ -247,6 +250,11 @@
             own(k, w)
 
     seqs = hidden.shape[0]
+    lane = lax.broadcasted_iota(jnp.int32, (1, HD), 1)
+    for s in range(seqs):
+        angles = lengths[s].astype(jnp.float32) * frequency[...]
+        cosine[s : s + 1, :] = jnp.cos(angles)
+        sine[s : s + 1, :] = jnp.where(lane < HD // 2, -jnp.sin(angles), jnp.sin(angles))
     tile = 128
     loads[0].wait()
 
@@ -274,6 +282,7 @@
         copy.wait()
 
     group = HQ // KVH
+    positions = k_held.shape[1]
     per_slot = joined.shape[2] // HD
     inv_root = 1.0 / jnp.sqrt(jnp.float32(HD))
 
@@ -300,7 +309,8 @@
 
     @pl.loop(0, seqs)
     def _(s):
-        is_live = live[pl.ds(s, 1), :] > 0.0
+        place = lax.broadcasted_iota(jnp.int32, (1, positions), 1) + tp * positions
+        is_live = place < lengths[s]
         for kv in range(KVH):
             at = slice(kv * HD, (kv + 1) * HD)
             lanes = slice(kv * PAD, (kv + 1) * PAD)
@@ -399,20 +409,41 @@
         copy.wait()
 
 
+def flush_kernel(decoded, qkv, out, decoded_to, qkv_to, out_to, sems):
+    copies = [pltpu.make_async_copy(decoded, decoded_to, sems.at[0])]
+    for source, target in ((qkv, qkv_to), (out, out_to)):
+        rows = source.shape[0] // CUTS
+        for i in range(CUTS):
+            at = pl.ds(i * rows, rows)
+            copies.append(
+                pltpu.make_async_copy(source.at[at], target.at[at], sems.at[len(copies)])
+            )
+    for copy in copies:
+        copy.start()
+    for copy in copies:
+        copy.wait()
+
+
+def flush(*arrays):
+    return pl.pallas_call(
+        flush_kernel,
+        out_shape=[jax.ShapeDtypeStruct(x.shape, x.dtype) for x in arrays],
+        in_specs=[pl.BlockSpec(memory_space=pltpu.VMEM)] * 3,
+        out_specs=[pl.BlockSpec(memory_space=pltpu.HBM)] * 3,
+        scratch_shapes=[pltpu.SemaphoreType.DMA((2 * CUTS + 1,))],
+        compiler_params=pltpu.CompilerParams(vmem_limit_bytes=2**20),
+    )(*arrays)
+
+
 def fused(mesh, hidden, lengths, old_qkv, old_out, keys, values, new_qkv, new_out):
     reps, tps = mesh.shape["rep"], mesh.shape["tp"]
     planes = reps // 2
-    seqs, positions = keys.shape[:2]
+    seqs = keys.shape[0]
     rows = new_qkv.shape[0]
     widths = (new_qkv.shape[1] // tps, new_out.shape[1] // tps)
     half = HD // 2
-    frequency = ROPE_BASE ** (-2.0 * jnp.arange(half, dtype=jnp.float32) / (2 * half))
-    angles = lengths.astype(jnp.float32)[:, None] * frequency
-    cosine, sine = jnp.cos(angles), jnp.sin(angles)
-    cosine = jnp.concatenate([cosine, cosine], axis=1)
-    sine = jnp.concatenate([-sine, sine], axis=1)
-    places = lax.axis_index("tp") * positions + jnp.arange(positions, dtype=jnp.int32)
-    live = (places[None, :] < lengths[:, None]).astype(jnp.float32)
+    frequency = ROPE_BASE ** (-2.0 * np.arange(half) / (2 * half))
+    frequency = jnp.asarray(np.concatenate([frequency, frequency])[None], jnp.float32)
 
     sem = pltpu.SemaphoreType.DMA
     whole, anywhere = pl.BlockSpec(memory_space=pltpu.VMEM), pl.BlockSpec(memory_space=pl.ANY)
@@ -432,18 +463,20 @@
         pltpu.VMEM((seqs, padded, HD), f32),
         pltpu.VMEM((tps, 3, seqs, padded, HD), f32),
         pltpu.VMEM((seqs, HQ * HD), bf16),
+        pltpu.VMEM((seqs, HD), f32),
+        pltpu.VMEM((seqs, HD), f32),
     ]
     return pl.pallas_call(
         functools.partial(step_kernel, planes, tps),
-        out_shape=[jax.ShapeDtypeStruct((seqs, widths[1]), bf16)]
+        out_shape=[pltpu.VMEM((seqs, widths[1]), bf16)]
         + [pltpu.VMEM((rows * reps * tps, width), bf16) for width in widths],
-        in_specs=[whole] * 4 + [in_hbm] * 6,
+        in_specs=[whole, pl.BlockSpec(memory_space=pltpu.SMEM), whole] + [in_hbm] * 6,
         out_specs=[whole] + [anywhere] * 2,
         scratch_shapes=scratch,
         compiler_params=pltpu.CompilerParams(
             collective_id=0, has_side_effects=True, vmem_limit_bytes=VMEM_BYTES - landed - SLACK
         ),
-    )(hidden, cosine, sine, live, old_qkv, old_out, keys, values, new_qkv, new_out)
+    )(hidden, lengths, frequency, old_qkv, old_out, keys, values, new_qkv, new_out)
 
 
 def solution(mesh):
@@ -465,7 +498,7 @@
         tiled = args[6].shape[0] % 16 == 0 and all(width % 128 == 0 for width in widths)
         if reps % 4 or not tiled:
             return (per_device(*args[:6]), *native_move(*args[6:]))
-        return tuple(fused(mesh, *args))
+        return tuple(flush(*fused(mesh, *args)))
 
     return jax.shard_map(
         step, mesh=mesh, in_specs=in_specs, out_specs=out_specs, check_vma=False

time: 139 us -> 135 us (0.971)
  local copies, waits for them, and re-layouts: 6.7 us -> 0 us
  Pallas kernels: 129 us -> 134 us
  other arithmetic: 2.77 us -> 0 us
    unnamed x5 -> x0, local copies, waits for them, and re-layouts: 6.7 us -> none
    pallas_call x1 -> x2, Pallas kernels: 129 us -> 134 us  [the longest x1 129 us: fused(): pl.pallas_call(functools.partial(step_kernel, planes, tps), out_shape=[pl...]
    convert_element_type x2 -> x0, other arithmetic: 1.98 us -> none  [the longest x1 1.32 us: fused(): live = (places[None, :] < lengths[:, None]).astype(jnp.float32)]
where the time goes in v3:
time: 135 us
  Pallas kernels  134 us (99%)
    pallas_call x1, Pallas kernels, fused(): pl.pallas_call(functools.partial(step_kernel, planes, tps), out_shape=[pl...  129 us
    pallas_call x1, Pallas kernels, flush(): pl.pallas_call(flush_kernel, out_shape=[jax.ShapeDtypeStruct(x.shape, x.d...  5.36 us

profile of v3, /device:TPU:0, one launch (start us, length us, event | category | flops | bytes accessed | tf_op | source)
XLA Modules:
  0.0 134.6 jit_solution(16818114676861125894)
XLA Ops:
  0.6 128.6 %shard_map.112 = (bf16[4,896]{1,0:T(4,128)(2,1)S(1)}, bf16[3584,1152]{1,0:T(8,128)(2,1)S(1)}, bf16[3584,896]{1,0:T(8,128)(2,1)S(1)}) custom-call(bf16[4,3584]{1,0:T(4,128)(2,1)} %hidden.1, s32[4]{0:T(128)} %lengths.1, f32[1,128]{1,0:T(1,128)} %constant.2.clone.frequency, bf16[3584,1152]{1,0:T(8,128)(2,1)} %old_qkv.1, bf16[3584,896]{1,0:T(8,128)(2,1)} %old_out.1, ...), custom_call_target="tpu_custom_call" | custom-call | tf_op jit(solution)/shard_map/pallas_call | solution.py:469
  129.2 5.4 %shard_map.113 = (bf16[4,896]{1,0:T(4,128)(2,1)}, bf16[3584,1152]{1,0:T(8,128)(2,1)}, bf16[3584,896]{1,0:T(8,128)(2,1)}) custom-call(bf16[4,896]{1,0:T(4,128)(2,1)S(1)} %get-tuple-element.6.decoded, bf16[3584,1152]{1,0:T(8,128)(2,1)S(1)} %get-tuple-element.7.qkv, bf16[3584,896]{1,0:T(8,128)(2,1)S(1)} %get-tuple-element.8.out), custom_call_target="tpu_custom_call" | custom-call | tf_op jit(solution)/shard_map/pallas_call | solution.py:428
